TPU v7x, 32 devices: a whole 2x2x4 slice. The times are simulated.
32 devices in a mesh: dom: 4 (over x, core), orient: 8 (over z, y).
Axes of the slice: x: 2, y: 2, z: 4, core: 2. Of those that a mesh axis runs over, the one named last changes fastest.
Arguments:
- particles: bfloat16 [2048, 2, 8192], P(('dom', 'orient')), may hold values from -48 to 48
- templates: bfloat16 [2048, 2, 8192], P('orient'), may hold values from -6 to 6
- tilt_low: int32 [2048], P(('dom', 'orient')), may hold values from 0 to 23
- tilt_high: int32 [2048], P(('dom', 'orient')), may hold values from 40 to 63
Outputs:
- updated: float32 [2048, 2, 8192], P('orient', None, 'dom')
- log_evidence: float32 [2048], P('dom')
All inputs are finite; a program needn't handle non-finite values.
Results may differ from a plain program's by a relative error of at most 0.0045.
Values may be sent and summed in bfloat16 or wider, within the bound.
A program may use at most 192 MiB of HBM per device.

v0:
```python
import math

import jax
import jax.numpy as jnp
from jax import lax
from jax.sharding import PartitionSpec as P

NBIN = 64


def bin_index(positions):
    return positions * 37 % NBIN


def on_device(particles, templates, tilt_low, tilt_high):
    bounds = jnp.stack([tilt_low, tilt_high], axis=1).astype(jnp.bfloat16)
    gathered, bound_rows = (
        lax.all_gather(particles, "orient", axis=0, tiled=True),
        lax.all_gather(bounds, "orient", axis=0, tiled=True),
    )
    lower_bin = bound_rows[:, 0].astype(jnp.int32)
    upper_bin = bound_rows[:, 1].astype(jnp.int32)
    group_rows = gathered.shape[0]
    band_size = gathered.shape[2]
    local_refs = templates.shape[0]
    inverse_temp = 3.0 / math.sqrt(band_size)
    binned = bin_index(jnp.arange(band_size, dtype=jnp.int32))
    observed = (
        (lower_bin[:, None] <= binned[None, :]) & (binned[None, :] < upper_bin[:, None])
    ).astype(jnp.bfloat16)
    masked = gathered * observed[:, None, :]
    flat_rows = masked.reshape(group_rows, 2 * band_size)
    template_flat = templates.reshape(local_refs, 2 * band_size)
    correlation = lax.dot_general(
        flat_rows, template_flat, (((1,), (1,)), ((), ())), preferred_element_type=jnp.float32
    )
    residue_mask = observed[:, :NBIN]
    real_part = templates[:, 0, :].astype(jnp.float32)
    imag_part = templates[:, 1, :].astype(jnp.float32)
    power = real_part * real_part + imag_part * imag_part
    residue_power = jnp.sum(power.reshape(local_refs, band_size // NBIN, NBIN), axis=1)
    penalty = jnp.dot(
        residue_mask.astype(jnp.float32), residue_power.T, precision=lax.Precision.HIGHEST
    )
    scores = inverse_temp * (correlation - 0.5 * penalty)
    local_peak = jnp.max(scores, axis=1)
    peak_score = lax.pmax(local_peak, "orient")
    total_mass = lax.psum(jnp.sum(jnp.exp(scores - peak_score[:, None]), axis=1), "orient")
    log_evidence = peak_score + jnp.log(total_mass)
    weights = jnp.exp(scores - log_evidence[:, None]).astype(jnp.bfloat16)
    numerator = lax.dot_general(
        weights, flat_rows, (((0,), (0,)), ((), ())), preferred_element_type=jnp.float32
    )
    numerator = numerator.reshape(local_refs, 2, band_size)
    dom_count = lax.axis_size("dom")
    slice_width = band_size // dom_count
    slice_start = lax.axis_index("dom") * slice_width
    previous = lax.dynamic_slice_in_dim(templates, slice_start, slice_width, 2).astype(jnp.float32)
    summed_num = lax.psum_scatter(
        numerator.astype(jnp.bfloat16), "dom", scatter_dimension=2, tiled=True
    ).astype(jnp.float32)
    residue_weights = lax.dot_general(
        weights, residue_mask, (((0,), (0,)), ((), ())), preferred_element_type=jnp.float32
    )
    residue_weights = lax.psum(residue_weights.astype(jnp.bfloat16), "dom").astype(jnp.float32)
    tiled_weights = jnp.tile(residue_weights, (1, band_size // NBIN))
    summed_den = lax.dynamic_slice_in_dim(tiled_weights, slice_start, slice_width, 1)[:, None, :]
    updated = (summed_num + previous) / (summed_den + 1.0)
    return (updated, log_evidence)


def solution(mesh):
    in_specs = (
        P(("dom", "orient"), None, None),
        P("orient", None, None),
        P(("dom", "orient")),
        P(("dom", "orient")),
    )
    out_specs = (P("orient", None, "dom"), P("dom"))
    return jax.shard_map(
        on_device, mesh=mesh, in_specs=in_specs, out_specs=out_specs, check_vma=False
    )
```

profile of v0, /device:TPU:0, one launch (start us, length us, event | category | flops | bytes accessed | tf_op | source)
XLA Modules:
  0.0 464.0 jit_solution(7442317399134628785)
XLA Ops:
  7.2 0.0 all-gather.3.cloned.1.call-start
  7.2 0.7 all-gather.3.cloned.1.call-update
  7.9 0.0 reduce-scatter.2.cloned.1.call-start
  7.9 0.7 convert_bitcast_fusion
  8.6 22.4 %all-gather = bf16[8,64,2]{1,2,0:T(2,128)(2,1)S(1)} all-gather(bf16[1,64,2]{1,2,0:T(2,128)(2,1)S(1)} %maximum_bitcast_fusion), channel_id=1, replica_groups=mesh['dom'=4,'orient'=8] {'orient'}, dimensions={0}, use_global_device_ids=true | all-gather | bytes 2304 | tf_op jit(solution)/shard_map/all_gather | solution.py:19
  31.1 0.1 reshape.97
  31.2 26.6 %fusion.16 = (bf16[256,1,8192]{2,1,0:T(2,128)(2,1)}, bf16[256,1,8192]{2,1,0:T(2,128)(2,1)}) fusion(bf16[256,2,8192]{2,1,0:T(2,128)(2,1)} %param.5), kind=kLoop, calls=%fused_computation.33 | loop fusion | bytes 16777216 | tf_op jit(solution)/shard_map/slice | solution.py:38
  57.8 17.3 %copy.30 = bf16[256,1,8192]{0,2,1:T(8,128)(2,1)} copy(bf16[256,1,8192]{2,1,0:T(2,128)(2,1)} %get-tuple-element.8) | data formatting | bytes 8388608
  75.1 17.2 %copy.31 = bf16[256,1,8192]{0,2,1:T(8,128)(2,1)} copy(bf16[256,1,8192]{2,1,0:T(2,128)(2,1)} %get-tuple-element.9) | data formatting | bytes 8388608
  92.3 8.9 %multiply_add_fusion = f32[256,1,8192]{0,2,1:T(8,128)} fusion(bf16[256,1,8192]{0,2,1:T(8,128)(2,1)} %copy.31, bf16[256,1,8192]{0,2,1:T(8,128)(2,1)} %copy.30), kind=kLoop, calls=%fused_computation.4 | loop fusion | flops 10485760 | bytes 16777216 | tf_op jit(solution)/shard_map/add | solution.py:40
  101.2 4.6 reduce_sum.18
  105.9 6.2 %compare_and_fusion = (pred[512,8192]{1,0:T(32,128)(4,1)}, bf16[512,8192]{1,0:T(8,128)(2,1)}) fusion(s32[8192]{0:T(1024)S(1)} %add_select_fusion, s32[512]{0:T(512)S(1)} %bitcast.30, s32[512]{0:T(512)S(1)} %bitcast.29), kind=kLoop, calls=%fused_computation.2 | loop fusion | flops 16777216 | bytes 12619776 | tf_op jit(solution)/shard_map/and | solution.py:29
  112.1 128.0 %all-gather.3.cloned.1.call-done = bf16[512,2,8192]{2,1,0:T(2,128)(2,1)} async-done(((bf16[64,2,8192]{2,1,0:T(2,128)(2,1)}), bf16[512,2,8192]{2,1,0:T(2,128)(2,1)}) %all-gather.3.cloned.1.call-update) | async-done | bytes 16777232 | tf_op jit(solution)/shard_map/all_gather | solution.py:18
  240.2 22.7 %broadcast_multiply_fusion = bf16[512,2,8192]{2,1,0:T(2,128)(2,1)} fusion(bf16[512,2,8192]{2,1,0:T(2,128)(2,1)} %all-gather.3.cloned.1.call-done, bf16[512,8192]{1,0:T(8,128)(2,1)} %get-tuple-element.11), kind=kLoop, calls=%fused_computation.5 | loop fusion | flops 8388608 | bytes 41943040 | tf_op jit(solution)/shard_map/mul | solution.py:31
  262.9 26.7 %fusion.4 = f32[512,256]{0,1:T(8,128)S(1)} fusion(bf16[512,2,8192]{2,1,0:T(2,128)(2,1)} %broadcast_multiply_fusion, bf16[256,2,8192]{2,1,0:T(2,128)(2,1)} %param.5), kind=kOutput, calls=%fused_computation.11 | convolution fusion | flops 4294967296 | bytes 25690112 | tf_op jit(solution)/shard_map/dot_general | solution.py:34
  289.6 1.2 fusion.17
  290.9 18.5 %pmax.7 = f32[512]{0:T(512)S(1)} all-reduce(f32[512]{0:T(512)S(1)} %get-tuple-element.14), channel_id=1, replica_groups=mesh['dom'=4,'orient'=8] {'orient'}, use_global_device_ids=true, to_apply=%region_2.3 | all-reduce | flops 512 | bytes 4096 | tf_op jit(solution)/shard_map/pmax | solution.py:47
  309.4 0.1 exponential_reduce_fusion
  309.5 17.8 %psum.14 = f32[512]{0:T(512)S(1)} all-reduce(f32[512]{0:T(512)S(1)} %exponential_reduce_fusion), channel_id=1, replica_groups=mesh['dom'=4,'orient'=8] {'orient'}, use_global_device_ids=true, to_apply=%region_4.5 | all-reduce | flops 512 | bytes 4096 | tf_op jit(solution)/shard_map/psum | solution.py:48
  327.3 0.0 copy-start
  327.3 18.5 %copy.32 = bf16[64,8,2,8192]{3,1,2,0:T(8,128)(2,1)} copy(bf16[64,8,2,8192]{3,2,1,0:T(2,128)(2,1)} %bitcast.24) | data formatting | bytes 33554432
  345.8 22.5 %copy.26 = bf16[16384,512]{1,0:T(8,128)(2,1)} copy(bf16[16384,512]{0,1:T(8,128)(2,1)} %bitcast.25) | data formatting | bytes 33554432 | tf_op jit(solution)/shard_map/dot_general | solution.py:51
  368.2 10.2 %convolution_convert_fusion = bf16[256,2,8192]{2,0,1:T(8,128)(2,1)} fusion(bf16[2,8192,512]{2,1,0:T(8,128)(2,1)} %bitcast.26, f32[512,256]{0,1:T(8,128)S(1)} %get-tuple-element.15, f32[512]{0:T(512)S(1)} %log_add_fusion), kind=kOutput, calls=%fused_computation.3 | convolution fusion | flops 4299423744 | bytes 25692160 | tf_op jit(solution)/shard_map/dot_general | solution.py:51
  378.5 0.0 reduce-scatter.2.cloned.1.call-update
  378.5 13.5 %copy.23 = bf16[256,2,8192]{2,0,1:T(8,128)(2,1)} copy(bf16[256,2,8192]{2,1,0:T(2,128)(2,1)} %param.5) | data formatting | bytes 16777216 | tf_op args[1]
  392.0 0.0 copy-done
  392.0 1.0 convolution_convert_fusion.1
  393.0 11.1 %psum.15 = bf16[256,64]{0,1:T(8,128)(2,1)S(1)} all-reduce(bf16[256,64]{0,1:T(8,128)(2,1)S(1)} %convolution_convert_fusion.1), channel_id=1, replica_groups=mesh['dom'=4,'orient'=8] {'dom'}, use_global_device_ids=true, to_apply=%region_6.7 | all-reduce | flops 16384 | bytes 65536 | tf_op jit(solution)/shard_map/psum | solution.py:65
  404.1 1.0 tile.4
  405.1 0.1 dynamic-slice_add_fusion
  405.3 1.8 copy.28
  407.1 41.0 %reduce-scatter.2.cloned.1.call-done = bf16[256,2,2048]{2,0,1:T(8,128)(2,1)} async-done(((bf16[256,2,8192]{2,0,1:T(8,128)(2,1)}), bf16[256,2,2048]{2,0,1:T(8,128)(2,1)}) %reduce-scatter.2.cloned.1.call-update) | async-done | bytes 2097168 | tf_op jit(solution)/shard_map/reduce_scatter | solution.py:59
  448.1 3.8 add_divide_fusion
  451.9 5.2 %copy.29 = f32[256,2,2048]{2,1,0:T(2,128)} copy(f32[256,2,2048]{2,0,1:T(8,128)S(1)} %add_divide_fusion) | data formatting | bytes 8388608
  (5 shorter events, 0.1 us)
Async XLA Ops:
  7.2 233.0 %all-gather.3.cloned.1.call-start = ((), (), s32[]{:S(2)}) async-start(), calls=%async_computation.1 | async-start | bytes 18874368 | tf_op jit(solution)/shard_map/all_gather | solution.py:18
  7.9 440.2 %reduce-scatter.2.cloned.1.call-start = ((), (), s32[]{:S(2)}) async-start(), calls=%async_computation.2 | async-start | bytes 10485760 | tf_op jit(solution)/shard_map/reduce_scatter | solution.py:59
  327.3 64.7 %copy-start = (f32[512]{0:T(512)}, f32[512]{0:T(512)S(1)}, u32[]{:S(2)}) copy-start(f32[512]{0:T(512)S(1)} %log_add_fusion) | copy-start | bytes 6148
Sparse Core Ops, SparseCore 0:
  10.1 230.0 all-gather.2
  378.6 69.4 reduce-scatter.1
where the time goes:
time: 466 us; the launch traced here: 464 us
  waiting for transfers between devices  170 us (36%)
  local copies, waits for them, and re-layouts  124 us (27%)
  blocking collectives  69.8 us (15%)
  other arithmetic  47.3 us (10%)
  matrix products  39.2 us (8%)
  between operations  14.1 us (3%)
    all_gather x1, waiting for transfers between devices, on_device(): lax.all_gather(particles, 'orient', axis=0, tiled=True)  128 us
    unnamed x8, local copies, waits for them, and re-layouts  71.8 us
    reduce_scatter x1, waiting for transfers between devices, on_device(): lax.psum_scatter(numerator.astype(jnp.bfloat16), 'dom', scatter_dimension...  41 us
    dot_general x1, matrix products, on_device(): lax.dot_general(flat_rows, template_flat, (((1,), (1,)), ((), ())), prefe...  26.7 us
    slice x1, local copies, waits for them, and re-layouts, on_device(): real_part = templates[:, 0, :].astype(jnp.float32)  26.6 us
    mul x1, other arithmetic, on_device(): masked = gathered * observed[:, None, :]  22.7 us
    dot_general x1, local copies, waits for them, and re-layouts, on_device(): lax.dot_general(weights, flat_rows, (((0,), (0,)), ((), ())), preferred_e...  22.5 us
    all_gather x1, blocking collectives, on_device(): lax.all_gather(bounds, 'orient', axis=0, tiled=True)  22.4 us
  transfers between devices with their start and end apart: 2, of which 2 were waited for; matrix products, arithmetic and copies ran while one was open for 21% of the time, Pallas kernels for 0%

commit v1 on v0

v1 whole, which is shorter than its diff:
```python
import functools
import math

import jax
import jax.numpy as jnp
from jax import lax
from jax.experimental import pallas as pl
from jax.experimental.pallas import tpu as pltpu
from jax.sharding import PartitionSpec as P

NBIN = 64
LANES = 128
MESH = pl.DeviceIdType.MESH


def bin_index(positions):
    return positions * 37 % NBIN


def kernel(
    doms, n, group, scale, xin_ref, t_ref, out_ref, lse_ref,
    x, part, score, stat, stat_all, wts, power,
    own_sem, x_send, x_recv, x_out, part_send, part_recv, stat_send, stat_recv,
):
    dom = lax.axis_index("dom")
    o = lax.axis_index("orient")
    line = n // 2
    a, b = o // 2, o % 2
    mate = a * 2 + (1 - b)
    rows, width = xin_ref.shape[1], xin_ref.shape[2]
    refs, body = t_ref.shape
    groups = n // group
    cols = group * doms * rows
    early = group == 1

    barrier = pltpu.get_barrier_semaphore()

    @pl.loop(1, doms)
    def _(i):
        pl.semaphore_signal(barrier, inc=1, device_id=(lax.rem(dom + i, doms), o), device_id_type=MESH)

    @pl.loop(1, n)
    def _(i):
        pl.semaphore_signal(barrier, inc=1, device_id=(dom, lax.rem(o + i, n)), device_id_type=MESH)

    pl.semaphore_wait(barrier, doms + n - 2)

    def spread(i):
        to = lax.rem(dom + i, doms)
        return pltpu.make_async_remote_copy(
            src_ref=xin_ref.at[to], dst_ref=x.at[o, dom],
            send_sem=x_out.at[i], recv_sem=x_recv.at[o, dom],
            device_id=(to, o), device_id_type=MESH,
        )

    own = pltpu.make_async_copy(xin_ref.at[dom], x.at[o, dom], own_sem)
    own.start()
    for i in range(1, doms):
        spread(i).start()

    def hop(direction, p, d, to):
        return pltpu.make_async_remote_copy(
            src_ref=x.at[p, d], dst_ref=x.at[p, d],
            send_sem=x_send.at[direction, p // 2, d], recv_sem=x_recv.at[p, d],
            device_id=(dom, to), device_id_type=MESH,
        )

    def arrive(p, d):
        hop(0, p, d, mate).wait_recv()

    def right(p, d):
        @pl.when(a + 1 < line)
        def _():
            hop(0, p, d, o + 2).start()

    def left(p, d):
        @pl.when(a > 0)
        def _():
            hop(1, p, d, o - 2).start()

    def across(p, d):
        hop(2, p, d, mate).start()

    def part_copy(g, i):
        return pltpu.make_async_remote_copy(
            src_ref=part.at[dom, g], dst_ref=part.at[dom, g],
            send_sem=part_send.at[i, g], recv_sem=part_recv.at[dom, g],
            device_id=(lax.rem(dom + i, doms), o), device_id_type=MESH,
        )

    def power_of():
        total = jnp.zeros((refs, LANES), jnp.float32)
        for j in range(body // LANES):
            piece = t_ref[:, j * LANES:(j + 1) * LANES].astype(jnp.float32)
            total = total + piece * piece
        total = total * -0.5
        high = total.astype(jnp.bfloat16)
        rest = total - high.astype(jnp.float32)
        middle = rest.astype(jnp.bfloat16)
        low = (rest - middle.astype(jnp.float32)).astype(jnp.bfloat16)
        power[0], power[1], power[2] = high, middle, low

    nt = (((1,), (1,)), ((), ()))

    def scores_of(g):
        block = x[pl.ds(g * group, group)].reshape(cols, width)
        seen = block[:, body:]
        total = lax.dot_general(t_ref[...], block[:, :body], nt, preferred_element_type=jnp.float32)
        for j in range(3):
            total = total + lax.dot_general(power[j], seen, nt, preferred_element_type=jnp.float32)
        part[dom, g] = total
        for i in range(1, doms):
            part_copy(g, i).start()

    power_of()
    own.wait()
    for i in range(doms):
        d = lax.rem(dom + i, doms)
        if i > 0:
            arrive(o, d)
        right(o, d)
        left(o, d)
        across(o, d)
    if early:
        scores_of(o)

    @pl.loop(1, line)
    def _(s):
        for i in range(doms):
            d = lax.rem(dom + i, doms)

            @pl.when(a - s >= 0)
            def _():
                p = o - 2 * s
                arrive(p, d)
                right(p, d)
                across(p, d)

            @pl.when(a + s < line)
            def _():
                p = o + 2 * s
                arrive(p, d)
                left(p, d)
                across(p, d)

        if early:
            for sign in (-1, 1):
                @pl.when((a + sign * s >= 0) & (a + sign * s < line))
                def _():
                    scores_of(o + 2 * sign * s)

    @pl.loop(0, 2 * line - 1)
    def _(j):
        s = (j + 1) // 2
        sign = 1 - 2 * (j % 2)
        at = a + sign * s

        @pl.when((at >= 0) & (at < line))
        def _():
            p = at * 2 + (1 - b)
            for i in range(doms):
                arrive(p, lax.rem(dom + i, doms))
            if early:
                scores_of(p)

    if not early:
        @pl.loop(0, groups)
        def _(g):
            scores_of(g)

    @pl.loop(0, groups)
    def _(g):
        for i in range(1, doms):
            d = lax.rem(dom + i, doms)
            pltpu.make_async_remote_copy(
                src_ref=part.at[d, g], dst_ref=part.at[d, g],
                send_sem=part_send.at[i, g], recv_sem=part_recv.at[d, g],
                device_id=(d, o), device_id_type=MESH,
            ).wait_recv()
        total = part[0, g]
        for d in range(1, doms):
            total = total + part[d, g]
        total = total * scale
        score[g] = total
        peak = jnp.max(total, axis=0, keepdims=True)
        stat[0, pl.ds(g, 1), :] = peak
        stat[1, pl.ds(g, 1), :] = jnp.sum(jnp.exp(total - peak), axis=0, keepdims=True)

    def stat_copy(i):
        return pltpu.make_async_remote_copy(
            src_ref=stat, dst_ref=stat_all.at[o],
            send_sem=stat_send.at[i], recv_sem=stat_recv.at[o],
            device_id=(dom, lax.rem(o + i, n)), device_id_type=MESH,
        )

    @pl.loop(1, n)
    def _(i):
        stat_copy(i).start()

    stat_all[o] = stat[...]

    @pl.loop(1, n)
    def _(i):
        p = lax.rem(o + i, n)
        pltpu.make_async_remote_copy(
            src_ref=stat, dst_ref=stat_all.at[p],
            send_sem=stat_send.at[i], recv_sem=stat_recv.at[p],
            device_id=(dom, p), device_id_type=MESH,
        ).wait_recv()

    top = stat_all[0, 0]
    for p in range(1, n):
        top = jnp.maximum(top, stat_all[p, 0])
    mass = jnp.zeros_like(top)
    for p in range(n):
        mass = mass + stat_all[p, 1] * jnp.exp(stat_all[p, 0] - top)
    lse_ref[...] = top + jnp.log(mass)

    for g in range(groups):
        wts[:, g * cols:(g + 1) * cols] = jnp.exp(score[g] - lse_ref[g:g + 1, :]).astype(jnp.bfloat16)

    nn = (((1,), (0,)), ((), ()))
    seen = x[:, :, :, body:].reshape(n * doms * rows, LANES)
    norm = 1.0 / (lax.dot_general(wts[...], seen, nn, preferred_element_type=jnp.float32) + 1.0)
    tile = 4 * LANES
    norm = jnp.concatenate([norm] * 4, axis=1)

    @pl.loop(0, body // tile)
    def _(j):
        at = pl.ds(pl.multiple_of(j * tile, tile), tile)
        piece = x[:, :, :, at].reshape(n * doms * rows, tile)
        num = lax.dot_general(wts[...], piece, nn, preferred_element_type=jnp.float32)
        out_ref[:, at] = (num + t_ref[:, at].astype(jnp.float32)) * norm

    for i in range(1, doms):
        spread(i).wait_send()

    @pl.loop(0, line)
    def _(q):
        p = q * 2 + b
        for d in range(doms):
            @pl.when((q <= a) & (a + 1 < line))
            def _():
                hop(0, p, d, mate).wait_send()

            @pl.when((q >= a) & (a > 0))
            def _():
                hop(1, p, d, mate).wait_send()

            hop(2, p, d, mate).wait_send()

    @pl.loop(0, groups)
    def _(g):
        for i in range(1, doms):
            part_copy(g, i).wait_send()

    @pl.loop(1, n)
    def _(i):
        stat_copy(i).wait_send()


def on_device(particles, templates, tilt_low, tilt_high):
    doms, n = lax.axis_size("dom"), lax.axis_size("orient")
    rows, _, band = particles.shape
    refs = templates.shape[0]
    part_band = band // doms
    body = 2 * part_band
    width = body + LANES
    group = max(1, 2 * LANES // (doms * rows))
    groups = n // group
    cols = group * doms * rows

    binned = bin_index(jnp.arange(band, dtype=jnp.int32))
    observed = (
        (tilt_low[:, None] <= binned[None, :]) & (binned[None, :] < tilt_high[:, None])
    ).astype(jnp.bfloat16)
    masked = particles * observed[:, None, :]
    masked = masked.reshape(rows, 2, doms, part_band).transpose(2, 0, 1, 3).reshape(doms, rows, body)
    seen = jnp.broadcast_to(observed[None, :, :LANES], (doms, rows, LANES))
    xin = jnp.concatenate([masked, seen], axis=2)
    start = lax.axis_index("dom") * part_band
    t = lax.dynamic_slice_in_dim(templates, start, part_band, 2).reshape(refs, body)

    vmem = pl.BlockSpec(memory_space=pltpu.VMEM)
    updated, lse = pl.pallas_call(
        functools.partial(kernel, doms, n, group, 3.0 / math.sqrt(band)),
        out_shape=(
            jax.ShapeDtypeStruct((refs, body), jnp.float32),
            jax.ShapeDtypeStruct((groups, cols), jnp.float32),
        ),
        in_specs=[vmem, vmem],
        out_specs=(vmem, vmem),
        scratch_shapes=[
            pltpu.VMEM((n, doms, rows, width), jnp.bfloat16),
            pltpu.VMEM((doms, groups, refs, cols), jnp.float32),
            pltpu.VMEM((groups, refs, cols), jnp.float32),
            pltpu.VMEM((2, groups, cols), jnp.float32),
            pltpu.VMEM((n, 2, groups, cols), jnp.float32),
            pltpu.VMEM((refs, n * doms * rows), jnp.bfloat16),
            pltpu.VMEM((3, refs, LANES), jnp.bfloat16),
            pltpu.SemaphoreType.DMA,
            pltpu.SemaphoreType.DMA((3, n // 2, doms)),
            pltpu.SemaphoreType.DMA((n, doms)),
            pltpu.SemaphoreType.DMA((doms,)),
            pltpu.SemaphoreType.DMA((doms, groups)),
            pltpu.SemaphoreType.DMA((doms, groups)),
            pltpu.SemaphoreType.DMA((n,)),
            pltpu.SemaphoreType.DMA((n,)),
        ],
        compiler_params=pltpu.CompilerParams(
            collective_id=0, has_side_effects=True, vmem_limit_bytes=60 * 2**20
        ),
    )(xin, t)
    mine = lax.dynamic_index_in_dim(
        lse.reshape(n, doms, rows), lax.axis_index("dom"), 1, keepdims=False
    )
    return updated.reshape(refs, 2, part_band), mine.reshape(n * rows)


def solution(mesh):
    in_specs = (
        P(("dom", "orient"), None, None),
        P("orient", None, None),
        P(("dom", "orient")),
        P(("dom", "orient")),
    )
    out_specs = (P("orient", None, "dom"), P("dom"))
    return jax.shard_map(
        on_device, mesh=mesh, in_specs=in_specs, out_specs=out_specs, check_vma=False
    )
```

time: 466 us -> 244 us (0.52)
  Pallas kernels: 0 us -> 216 us
  waiting for transfers between devices: 170 us -> 0 us
  local copies, waits for them, and re-layouts: 124 us -> 18.8 us
  blocking collectives: 69.8 us -> 0 us
  other arithmetic: 47.3 us -> 6.64 us
  matrix products: 39.2 us -> 0 us
  between operations: 14.1 us -> 0.7 us
    pallas_call x0 -> x1, Pallas kernels: none -> 216 us  [on_device(): pl.pallas_call(functools.partial(kernel, doms, n, group, 3.0 / math.sqrt(...]
    all_gather x1 -> x0, waiting for transfers between devices: 128 us -> none  [on_device(): lax.all_gather(particles, 'orient', axis=0, tiled=True)]
    unnamed x8 -> x3, local copies, waits for them, and re-layouts: 71.8 us -> 2.22 us
    reduce_scatter x1 -> x0, waiting for transfers between devices: 41 us -> none  [on_device(): lax.psum_scatter(numerator.astype(jnp.bfloat16), 'dom', scatter_dimension...]
    dot_general x4 -> x0, matrix products: 39.2 us -> none  [the longest x1 26.7 us: on_device(): lax.dot_general(flat_rows, template_flat, (((1,), (1,)), ((), ())), prefe...]
    psum x2 -> x0, blocking collectives: 28.8 us -> none  [the longest x1 17.8 us: on_device(): lax.psum(jnp.sum(jnp.exp(scores - peak_score[:, None]), axis=1), 'orient')]
    slice x1, local copies, waits for them, and re-layouts: 26.6 us -> 0.01 us  [on_device(): seen = jnp.broadcast_to(observed[None, :, :LANES], (doms, rows, LANES))]
    dot_general x1 -> x0, local copies, waits for them, and re-layouts: 22.5 us -> none  [on_device(): lax.dot_general(weights, flat_rows, (((0,), (0,)), ((), ())), preferred_e...]
  transfers between devices with their start and end apart: 2 -> 0, of which waited for: 2 -> 0; matrix products, arithmetic and copies ran while one was open for 21% -> 0% of each run, Pallas kernels for 0% -> 0%
where the time goes in v1:
time: 244 us; the launch traced here: 242 us
  Pallas kernels  216 us (89%)
  local copies, waits for them, and re-layouts  18.8 us (8%)
  other arithmetic  6.64 us (3%)
    pallas_call x1, Pallas kernels, on_device(): pl.pallas_call(functools.partial(kernel, doms, n, group, 3.0 / math.sqrt(...  216 us
    reshape x2, local copies, waits for them, and re-layouts, on_device(): return (updated.reshape(refs, 2, part_band), mine.reshape(n * rows))  7.22 us
    reshape x2, local copies, waits for them, and re-layouts, on_device(): masked.reshape(rows, 2, doms, part_band).transpose(2, 0, 1, 3)  6.22 us

profile of v1, /device:TPU:0, one launch (start us, length us, event | category | flops | bytes accessed | tf_op | source)
XLA Modules:
  0.0 242.1 jit_solution(18060397967861019969)
XLA Ops:
  0.7 1.0 and_convert_fusion
  1.7 4.0 %broadcast_multiply_fusion = bf16[64,2,8192]{2,1,0:T(2,128)(2,1)S(1)} fusion(bf16[64,2,8192]{2,1,0:T(2,128)(2,1)} %param.4, bf16[64,8192]{1,0:T(8,128)(2,1)S(1)} %and_convert_fusion), kind=kLoop, calls=%fused_computation.3 | loop fusion | flops 1048576 | bytes 5242880 | tf_op jit(solution)/shard_map/mul | solution.py:277
  5.8 2.9 %copy.10 = bf16[64,1,4,2,2048]{4,3,1,0,2:T(2,128)(2,1)} copy(bf16[64,1,4,2,2048]{4,3,2,1,0:T(2,128)(2,1)S(1)} %bitcast.10) | data formatting | bytes 4194304 | tf_op jit(solution)/shard_map/reshape | solution.py:278
  8.7 3.3 %reshape.88 = bf16[4,64,4096]{2,1,0:T(8,128)(2,1)S(1)} reshape(bf16[4,64,2,2048]{3,2,1,0:T(2,128)(2,1)} %bitcast.11) | data formatting | bytes 4194304 | tf_op jit(solution)/shard_map/reshape | solution.py:278
  12.0 1.6 pad_maximum_fusion.xin_ref
  13.6 3.0 %constant_dynamic-slice_fusion = bf16[256,2,2048]{2,1,0:T(2,128)(2,1)S(1)} fusion(bf16[256,2,8192]{2,1,0:T(2,128)(2,1)} %param.5, s32[]{:T(128)S(6)} %select_n.21), kind=kLoop, calls=%fused_computation.12 | loop fusion | bytes 4194308 | tf_op jit(solution)/shard_map/dynamic_slice | solution.py:282
  16.6 2.2 copy.8
  18.8 216.0 %shard_map.59 = (f32[256,4096]{1,0:T(8,128)}, f32[8,256]{1,0:T(8,128)}) custom-call(bf16[4,64,4224]{2,1,0:T(8,128)(2,1)} %pad_maximum_fusion.xin_ref, bf16[256,4096]{1,0:T(8,128)(2,1)} %bitcast.9), custom_call_target="tpu_custom_call" | custom-call | tf_op jit(solution)/shard_map/pallas_call | solution.py:285
  234.8 0.0 copy-start
  234.8 6.6 %reshape.90 = f32[256,2,2048]{2,1,0:T(2,128)} reshape(f32[256,4096]{1,0:T(8,128)} %get-tuple-element.4) | data formatting | bytes 8388608 | tf_op jit(solution)/shard_map/reshape | solution.py:317
  241.4 0.0 copy-done
  241.4 0.1 reshape.91
  241.5 0.7 reshape.92
  (4 shorter events, 0.1 us)
Async XLA Ops:
  234.8 6.6 %copy-start = (f32[8,256]{1,0:T(8,128)S(1)}, f32[8,256]{1,0:T(8,128)}, u32[]{:S(2)}) copy-start(f32[8,256]{1,0:T(8,128)} %get-tuple-element.5) | copy-start | bytes 24580

commit v2 on v1

--- a/solution.py
+++ b/solution.py
@@ -18,9 +18,9 @@
 
 
 def kernel(
-    doms, n, group, scale, xin_ref, t_ref, out_ref, lse_ref,
-    x, part, score, stat, stat_all, wts, power,
-    own_sem, x_send, x_recv, x_out, part_send, part_recv, stat_send, stat_recv,
+    doms, n, group, scale, raw_ref, seen_ref, tall_ref, out_ref, lse_ref,
+    xin_ref, t_raw, t_ref, x, part, score, stat, stat_all, wts, power,
+    t_sem, own_sem, x_send, relay_send, x_recv, x_out, part_send, part_recv, stat_send, stat_recv,
 ):
     dom = lax.axis_index("dom")
     o = lax.axis_index("orient")
@@ -32,6 +32,14 @@
     groups = n // group
     cols = group * doms * rows
     early = group == 1
+    stages = doms.bit_length() - 1
+    half = line // 2
+
+    kd = body // 2
+    t_copy = pltpu.make_async_copy(
+        tall_ref.at[:, :, pl.ds(pl.multiple_of(dom * kd, kd), kd)], t_raw, t_sem
+    )
+    t_copy.start()
 
     barrier = pltpu.get_barrier_semaphore()
 
@@ -42,6 +50,12 @@
     @pl.loop(1, n)
     def _(i):
         pl.semaphore_signal(barrier, inc=1, device_id=(dom, lax.rem(o + i, n)), device_id_type=MESH)
+
+    xin_ref[:, :, body:] = jnp.broadcast_to(seen_ref[...][None], (doms, rows, LANES))
+    tiled = jnp.concatenate([seen_ref[...]] * (kd // LANES), axis=1)
+    for d in range(doms):
+        for c in range(2):
+            xin_ref[d, :, c * kd:(c + 1) * kd] = raw_ref[:, c, d * kd:(d + 1) * kd] * tiled
 
     pl.semaphore_wait(barrier, doms + n - 2)
 
@@ -78,14 +92,47 @@
         def _():
             hop(1, p, d, o - 2).start()
 
-    def across(p, d):
-        hop(2, p, d, mate).start()
-
-    def part_copy(g, i):
-        return pltpu.make_async_remote_copy(
-            src_ref=part.at[dom, g], dst_ref=part.at[dom, g],
-            send_sem=part_send.at[i, g], recv_sem=part_recv.at[dom, g],
-            device_id=(lax.rem(dom + i, doms), o), device_id_type=MESH,
+    def relayed(at, q, i):
+        late = i >= doms // 2
+        inner = ((q == at + 1) & (at >= half) & (at < line - 1)) | ((q == at - 1) & (at < half) & (at > 0))
+        outer = ((q == at - 1) & (at == line - 1)) | ((q == at + 1) & (at == 0))
+        return (inner | outer) if late else inner
+
+    def across(p, d, i):
+        @pl.when(jnp.logical_not(relayed(a, p // 2, i)))
+        def _():
+            hop(2, p, d, mate).start()
+
+    def relay(d, i):
+        for sign in (1, -1):
+            @pl.when((a + sign >= 0) & (a + sign < line) & relayed(a + sign, a, i))
+            def _():
+                relay_copy(sign, d).start()
+
+    def relay_copy(sign, d):
+        return pltpu.make_async_remote_copy(
+            src_ref=x.at[mate, d], dst_ref=x.at[mate, d],
+            send_sem=relay_send.at[(1 - sign) // 2, d], recv_sem=x_recv.at[mate, d],
+            device_id=(dom, o + 2 * sign), device_id_type=MESH,
+        )
+
+    def from_mate(s):
+        for sign in (-1, 1):
+            @pl.when((a + sign * s >= 0) & (a + sign * s < line))
+            def _():
+                p = mate + 2 * sign * s
+                for i in range(doms):
+                    arrive(p, lax.rem(dom + i, doms))
+                if early:
+                    scores_of(p)
+
+    def part_copy(g, k):
+        step = 2 ** k
+        flip = dom + step - 2 * step * (dom // step % 2)
+        return pltpu.make_async_remote_copy(
+            src_ref=part.at[2 * k, g], dst_ref=part.at[2 * k + 1, g],
+            send_sem=part_send.at[k, g], recv_sem=part_recv.at[k, g],
+            device_id=(flip, o), device_id_type=MESH,
         )
 
     def power_of():
@@ -108,11 +155,13 @@
         total = lax.dot_general(t_ref[...], block[:, :body], nt, preferred_element_type=jnp.float32)
         for j in range(3):
             total = total + lax.dot_general(power[j], seen, nt, preferred_element_type=jnp.float32)
-        part[dom, g] = total
-        for i in range(1, doms):
-            part_copy(g, i).start()
-
-    power_of()
+        part[0, g] = total
+        part_copy(g, 0).start()
+        for k in range(1, stages):
+            part_copy(g, k - 1).wait_recv()
+            part[2 * k, g] = part[2 * k - 2, g] + part[2 * k - 1, g]
+            part_copy(g, k).start()
+
     own.wait()
     for i in range(doms):
         d = lax.rem(dom + i, doms)
@@ -120,7 +169,17 @@
             arrive(o, d)
         right(o, d)
         left(o, d)
-        across(o, d)
+        across(o, d, i)
+    t_copy.wait()
+    step = 32
+
+    @pl.loop(0, refs // step)
+    def _(j):
+        at = pl.ds(pl.multiple_of(j * step, step), step)
+        for c in range(2):
+            t_ref[at, c * kd:(c + 1) * kd] = t_raw[at, c, :]
+
+    power_of()
     if early:
         scores_of(o)
 
@@ -134,14 +193,14 @@
                 p = o - 2 * s
                 arrive(p, d)
                 right(p, d)
-                across(p, d)
+                across(p, d, i)
 
             @pl.when(a + s < line)
             def _():
                 p = o + 2 * s
                 arrive(p, d)
                 left(p, d)
-                across(p, d)
+                across(p, d, i)
 
         if early:
             for sign in (-1, 1):
@@ -149,19 +208,20 @@
                 def _():
                     scores_of(o + 2 * sign * s)
 
-    @pl.loop(0, 2 * line - 1)
-    def _(j):
-        s = (j + 1) // 2
-        sign = 1 - 2 * (j % 2)
-        at = a + sign * s
-
-        @pl.when((at >= 0) & (at < line))
-        def _():
-            p = at * 2 + (1 - b)
+        @pl.when(s == 1)
+        def _():
             for i in range(doms):
-                arrive(p, lax.rem(dom + i, doms))
+                d = lax.rem(dom + i, doms)
+                arrive(mate, d)
+                relay(d, i)
             if early:
-                scores_of(p)
+                scores_of(mate)
+
+        @pl.when(s > 1)
+        def _():
+            from_mate(s - 1)
+
+    from_mate(line - 1)
 
     if not early:
         @pl.loop(0, groups)
@@ -170,16 +230,8 @@
 
     @pl.loop(0, groups)
     def _(g):
-        for i in range(1, doms):
-            d = lax.rem(dom + i, doms)
-            pltpu.make_async_remote_copy(
-                src_ref=part.at[d, g], dst_ref=part.at[d, g],
-                send_sem=part_send.at[i, g], recv_sem=part_recv.at[d, g],
-                device_id=(d, o), device_id_type=MESH,
-            ).wait_recv()
-        total = part[0, g]
-        for d in range(1, doms):
-            total = total + part[d, g]
+        part_copy(g, stages - 1).wait_recv()
+        total = part[2 * stages - 2, g] + part[2 * stages - 1, g]
         total = total * scale
         score[g] = total
         peak = jnp.max(total, axis=0, keepdims=True)
@@ -238,7 +290,9 @@
     @pl.loop(0, line)
     def _(q):
         p = q * 2 + b
-        for d in range(doms):
+        for i in range(doms):
+            d = lax.rem(dom + i, doms)
+
             @pl.when((q <= a) & (a + 1 < line))
             def _():
                 hop(0, p, d, mate).wait_send()
@@ -247,12 +301,21 @@
             def _():
                 hop(1, p, d, mate).wait_send()
 
-            hop(2, p, d, mate).wait_send()
+            @pl.when(jnp.logical_not(relayed(a, q, i)))
+            def _():
+                hop(2, p, d, mate).wait_send()
+
+    for i in range(doms):
+        d = lax.rem(dom + i, doms)
+        for sign in (1, -1):
+            @pl.when((a + sign >= 0) & (a + sign < line) & relayed(a + sign, a, i))
+            def _():
+                relay_copy(sign, d).wait_send()
 
     @pl.loop(0, groups)
     def _(g):
-        for i in range(1, doms):
-            part_copy(g, i).wait_send()
+        for k in range(stages):
+            part_copy(g, k).wait_send()
 
     @pl.loop(1, n)
     def _(i):
@@ -269,18 +332,12 @@
     group = max(1, 2 * LANES // (doms * rows))
     groups = n // group
     cols = group * doms * rows
-
-    binned = bin_index(jnp.arange(band, dtype=jnp.int32))
-    observed = (
+    stages = doms.bit_length() - 1
+
+    binned = bin_index(jnp.arange(LANES, dtype=jnp.int32))
+    seen = (
         (tilt_low[:, None] <= binned[None, :]) & (binned[None, :] < tilt_high[:, None])
     ).astype(jnp.bfloat16)
-    masked = particles * observed[:, None, :]
-    masked = masked.reshape(rows, 2, doms, part_band).transpose(2, 0, 1, 3).reshape(doms, rows, body)
-    seen = jnp.broadcast_to(observed[None, :, :LANES], (doms, rows, LANES))
-    xin = jnp.concatenate([masked, seen], axis=2)
-    start = lax.axis_index("dom") * part_band
-    t = lax.dynamic_slice_in_dim(templates, start, part_band, 2).reshape(refs, body)
-
     vmem = pl.BlockSpec(memory_space=pltpu.VMEM)
     updated, lse = pl.pallas_call(
         functools.partial(kernel, doms, n, group, 3.0 / math.sqrt(band)),
@@ -288,29 +345,34 @@
             jax.ShapeDtypeStruct((refs, body), jnp.float32),
             jax.ShapeDtypeStruct((groups, cols), jnp.float32),
         ),
-        in_specs=[vmem, vmem],
+        in_specs=[vmem, vmem, pl.BlockSpec(memory_space=pl.ANY)],
         out_specs=(vmem, vmem),
         scratch_shapes=[
+            pltpu.VMEM((doms, rows, width), jnp.bfloat16),
+            pltpu.VMEM((refs, 2, part_band), jnp.bfloat16),
+            pltpu.VMEM((refs, body), jnp.bfloat16),
             pltpu.VMEM((n, doms, rows, width), jnp.bfloat16),
-            pltpu.VMEM((doms, groups, refs, cols), jnp.float32),
+            pltpu.VMEM((2 * stages, groups, refs, cols), jnp.float32),
             pltpu.VMEM((groups, refs, cols), jnp.float32),
             pltpu.VMEM((2, groups, cols), jnp.float32),
             pltpu.VMEM((n, 2, groups, cols), jnp.float32),
             pltpu.VMEM((refs, n * doms * rows), jnp.bfloat16),
             pltpu.VMEM((3, refs, LANES), jnp.bfloat16),
             pltpu.SemaphoreType.DMA,
+            pltpu.SemaphoreType.DMA,
             pltpu.SemaphoreType.DMA((3, n // 2, doms)),
+            pltpu.SemaphoreType.DMA((2, doms)),
             pltpu.SemaphoreType.DMA((n, doms)),
             pltpu.SemaphoreType.DMA((doms,)),
-            pltpu.SemaphoreType.DMA((doms, groups)),
-            pltpu.SemaphoreType.DMA((doms, groups)),
+            pltpu.SemaphoreType.DMA((stages, groups)),
+            pltpu.SemaphoreType.DMA((stages, groups)),
             pltpu.SemaphoreType.DMA((n,)),
             pltpu.SemaphoreType.DMA((n,)),
         ],
         compiler_params=pltpu.CompilerParams(
             collective_id=0, has_side_effects=True, vmem_limit_bytes=60 * 2**20
         ),
-    )(xin, t)
+    )(particles, seen, templates)
     mine = lax.dynamic_index_in_dim(
         lse.reshape(n, doms, rows), lax.axis_index("dom"), 1, keepdims=False
     )

time: 244 us -> 225 us (0.922)
  local copies, waits for them, and re-layouts: 18.8 us -> 8.01 us
  other arithmetic: 6.64 us -> 1.37 us
    reshape x2 -> x0, local copies, waits for them, and re-layouts: 6.22 us -> none  [on_device(): masked.reshape(rows, 2, doms, part_band).transpose(2, 0, 1, 3)]
    mul x1 -> x0, other arithmetic: 4.02 us -> none  [on_device(): masked = particles * observed[:, None, :]]
    dynamic_slice x1 -> x0, local copies, waits for them, and re-layouts: 3.03 us -> none  [on_device(): lax.dynamic_slice_in_dim(templates, start, part_band, 2).reshape(refs, body)]
where the time goes in v2:
time: 225 us
  Pallas kernels  215 us (96%)
  local copies, waits for them, and re-layouts  8.01 us (4%)
    pallas_call x1, Pallas kernels, on_device(): pl.pallas_call(functools.partial(kernel, doms, n, group, 3.0 / math.sqrt(...  215 us
    reshape x2, local copies, waits for them, and re-layouts, on_device(): return (updated.reshape(refs, 2, part_band), mine.reshape(n * rows))  7.22 us

profile of v2, /device:TPU:0, one launch (start us, length us, event | category | flops | bytes accessed | tf_op | source)
XLA Modules:
  0.0 225.0 jit_solution(9867838551181745586)
XLA Ops:
  0.6 1.4 and_convert_fusion.seen_ref
  2.0 214.9 %shard_map.59 = (f32[256,4096]{1,0:T(8,128)}, f32[8,256]{1,0:T(8,128)}) custom-call(bf16[64,2,8192]{2,1,0:T(2,128)(2,1)} %raw_ref.1, bf16[64,128]{1,0:T(8,128)(2,1)} %and_convert_fusion.seen_ref, bf16[256,2,8192]{2,1,0:T(2,128)(2,1)} %tall_ref.1), custom_call_target="tpu_custom_call" | custom-call | tf_op jit(solution)/shard_map/pallas_call | solution.py:342
  217.0 0.8 reshape.32
  217.8 0.7 reshape.33
  218.4 6.6 %reshape.31 = f32[256,2,2048]{2,1,0:T(2,128)} reshape(f32[256,4096]{1,0:T(8,128)} %get-tuple-element.4) | data formatting | bytes 8388608 | tf_op jit(solution)/shard_map/reshape | solution.py:379
  (2 shorter events, 0.0 us)
